TPU v7x, 32 devices: a whole 2x2x4 slice. The times are simulated.
32 devices in a mesh: row: 8 (over z, y), col: 4 (over x, core).
Axes of the slice: x: 2, y: 2, z: 4, core: 2. Of those that a mesh axis runs over, the one named last changes fastest.
Arguments:
- matrix: bfloat16 [32768, 32768], P('row', 'col'), may hold values from -0.03125 to 0.03125
- right_sides: float32 [32768, 64], P(('row', 'col')), may hold values from -6 to 6
- initial_guess: float32 [32768, 64], P(('row', 'col')), may hold values from -6 to 6
Outputs:
- solution: float32 [32768, 64], P(('row', 'col'))
All inputs are finite; a program needn't handle non-finite values.
Results may differ from a plain program's by a relative error of at most 0.0038.
Values may be sent and summed in bfloat16 or wider, within the bound.
A program may use at most 128 MiB of HBM per device.

v0:
```python
import jax
import jax.numpy as jnp
from jax import lax
from jax.sharding import PartitionSpec as P

STEPS = 3


DIAGONAL_SHIFT = 1.4


def inner_products(left, right):
    return jnp.einsum("rk,rs->ks", left, right, precision=lax.Precision.HIGHEST)


def combine_basis(stacked, weights):
    return jnp.dot(stacked, weights, precision=lax.Precision.HIGHEST)


def orthonormal(applied, gram_sum):
    lower_factor = jnp.linalg.cholesky(gram_sum)
    basis_next = lax.linalg.triangular_solve(
        lower_factor, applied, left_side=False, lower=True, transpose_a=True
    )
    return (basis_next, lower_factor.T)


def least_squares(column_list, top_factor):
    span_width = top_factor.shape[0]
    count = len(column_list)
    pieces = []
    for position, (projected, upper_factor) in enumerate(column_list):
        filler = jnp.zeros(((count - position - 1) * span_width, span_width), jnp.float32)
        pieces.append(jnp.concatenate([projected, upper_factor, filler], axis=0))
    hessenberg = jnp.concatenate(pieces, axis=1)
    normal_matrix = inner_products(hessenberg, hessenberg)
    target = inner_products(hessenberg[:span_width], top_factor)
    lower_factor = jnp.linalg.cholesky(normal_matrix)
    halfway = lax.linalg.triangular_solve(lower_factor, target, left_side=True, lower=True)
    return lax.linalg.triangular_solve(
        lower_factor, halfway, left_side=True, lower=True, transpose_a=True
    )


def per_device(matrix, right_sides, initial_guess):

    def fold_panel(panel_piece):
        return jnp.dot(matrix, panel_piece, preferred_element_type=jnp.float32)

    def operate(local_block):
        operand = local_block.astype(jnp.bfloat16)
        partial_sum = fold_panel(lax.all_gather(operand, "row", axis=0, tiled=True))
        product = lax.psum_scatter(partial_sum, "col", scatter_dimension=0, tiled=True)
        return DIAGONAL_SHIFT * local_block + product

    def reduce_all(local_sum):
        return lax.psum(local_sum, ("row", "col"))

    guess_local, sides_local = (initial_guess, right_sides)
    residual_start = sides_local - operate(guess_local)
    basis_now, top_factor = orthonormal(
        residual_start, reduce_all(inner_products(residual_start, residual_start))
    )
    basis_list = [basis_now]
    column_list = []
    for iteration in range(STEPS):
        applied = operate(basis_list[-1])
        stacked = jnp.concatenate(basis_list, axis=1)
        span_width = stacked.shape[1]
        combined = reduce_all(inner_products(jnp.concatenate([stacked, applied], axis=1), applied))
        projected = combined[:span_width]
        gram_sum = combined[span_width:] - inner_products(projected, projected)
        applied = applied - combine_basis(stacked, projected)
        basis_now, upper_factor = orthonormal(applied, gram_sum)
        basis_list.append(basis_now)
        column_list.append((projected, upper_factor))
    coefficients = least_squares(column_list, top_factor)
    update = combine_basis(jnp.concatenate(basis_list[:-1], axis=1), coefficients)
    return guess_local + update


def solution(mesh):
    return jax.shard_map(
        per_device,
        mesh=mesh,
        in_specs=(P("row", "col"), P(("row", "col"), None), P(("row", "col"), None)),
        out_specs=P(("row", "col"), None),
        check_vma=False,
    )
```

profile of v0, /device:TPU:1, one launch (start us, length us, event | category | flops | bytes accessed | tf_op | source)
XLA Modules:
  0.0 751.0 jit_solution(7809911143641430685)
XLA Ops:
  6.5 1.7 convert_element_type.12
  8.3 41.9 %all-gather.5.cloned.1.call-done = bf16[8192,64]{0,1:T(8,128)(2,1)} async-done(((bf16[1024,64]{0,1:T(8,128)(2,1)}), bf16[8192,64]{0,1:T(8,128)(2,1)}) %all-gather.5.cloned.1.call-update) | async-done | bytes 1048592 | tf_op jit(solution)/shard_map/all_gather | solution.py:52
  50.2 29.6 %fusion.97 = f32[4096,64]{0,1:T(8,128)} fusion(bf16[4096,8192]{1,0:T(8,128)(2,1)} %param.6, bf16[8192,64]{0,1:T(8,128)(2,1)} %all-gather.5.cloned.1.call-done), kind=kOutput, calls=%fused_computation.157 | convolution fusion | flops 4294967296 | bytes 69206016 | tf_op jit(solution)/shard_map/dot_general | solution.py:48
  79.9 25.2 %reduce-scatter.5.cloned.1.call-done = f32[1024,64]{0,1:T(8,128)} async-done(((f32[4096,64]{0,1:T(8,128)}), f32[1024,64]{0,1:T(8,128)}) %reduce-scatter.5.cloned.1.call-update) | async-done | bytes 262160 | tf_op jit(solution)/shard_map/reduce_scatter | solution.py:53
  105.0 1.4 fusion.93
  106.5 38.8 %psum.28 = f32[64,64]{0,1:T(8,128)S(1)} all-reduce(f32[64,64]{0,1:T(8,128)S(1)} %fusion.93), channel_id=1, replica_groups=mesh['row'=8,'col'=4] {'row','col'}, use_global_device_ids=true, to_apply=%region_1.0 | all-reduce | flops 4096 | bytes 32768 | tf_op jit(solution)/shard_map/psum | solution.py:57
  145.4 5.8 cholesky.195
  152.6 4.9 custom-call.25
  157.5 2.0 fusion.94
  159.6 40.1 %all-gather.7.cloned.1.call-done = bf16[8192,64]{0,1:T(8,128)(2,1)} async-done(((bf16[1024,64]{0,1:T(8,128)(2,1)}), bf16[8192,64]{0,1:T(8,128)(2,1)}) %all-gather.7.cloned.1.call-update) | async-done | bytes 1048592 | tf_op jit(solution)/shard_map/all_gather | solution.py:52
  199.7 28.4 %convolution_bitcast_fusion.2 = f32[4096,64]{0,1:T(8,128)} fusion(bf16[8192,64]{0,1:T(8,128)(2,1)} %all-gather.7.cloned.1.call-done, bf16[4096,8192]{1,0:T(8,128)(2,1)} %param.6), kind=kOutput, calls=%fused_computation.2 | convolution fusion | flops 4294967296 | bytes 69206016 | tf_op jit(solution)/shard_map/dot_general | solution.py:48
  228.2 25.1 %reduce-scatter.7.cloned.1.call-done = f32[1024,64]{0,1:T(8,128)} async-done(((f32[4096,64]{0,1:T(8,128)}), f32[1024,64]{0,1:T(8,128)}) %reduce-scatter.7.cloned.1.call-update) | async-done | bytes 262160 | tf_op jit(solution)/shard_map/reduce_scatter | solution.py:53
  255.0 39.0 %psum.29 = f32[128,64]{0,1:T(8,128)S(1)} all-reduce(f32[128,64]{0,1:T(8,128)S(1)} %fusion.13), channel_id=1, replica_groups=mesh['row'=8,'col'=4] {'row','col'}, use_global_device_ids=true, to_apply=%region_5.8 | all-reduce | flops 8192 | bytes 65536 | tf_op jit(solution)/shard_map/psum | solution.py:57
  294.3 5.8 cholesky.206
  301.5 4.9 custom-call.26
  308.9 40.2 %all-gather.9.cloned.1.call-done = bf16[8192,64]{0,1:T(8,128)(2,1)} async-done(((bf16[1024,64]{0,1:T(8,128)(2,1)}), bf16[8192,64]{0,1:T(8,128)(2,1)}) %all-gather.9.cloned.1.call-update) | async-done | bytes 1048592 | tf_op jit(solution)/shard_map/all_gather | solution.py:52
  349.1 28.4 %convolution_bitcast_fusion.1 = f32[4096,64]{0,1:T(8,128)} fusion(bf16[8192,64]{0,1:T(8,128)(2,1)} %all-gather.9.cloned.1.call-done, bf16[4096,8192]{1,0:T(8,128)(2,1)} %param.6), kind=kOutput, calls=%fused_computation.1 | convolution fusion | flops 4294967296 | bytes 69206016 | tf_op jit(solution)/shard_map/dot_general | solution.py:48
  377.6 25.2 %reduce-scatter.9.cloned.1.call-done = f32[1024,64]{0,1:T(8,128)} async-done(((f32[4096,64]{0,1:T(8,128)}), f32[1024,64]{0,1:T(8,128)}) %reduce-scatter.9.cloned.1.call-update) | async-done | bytes 262160 | tf_op jit(solution)/shard_map/reduce_scatter | solution.py:53
  404.6 39.0 %psum.30 = f32[192,64]{0,1:T(8,128)S(1)} all-reduce(f32[192,64]{0,1:T(8,128)S(1)} %fusion.8), channel_id=1, replica_groups=mesh['row'=8,'col'=4] {'row','col'}, use_global_device_ids=true, to_apply=%region_7.10 | all-reduce | flops 12288 | bytes 98304 | tf_op jit(solution)/shard_map/psum | solution.py:57
  443.8 5.8 cholesky.217
  451.0 4.9 custom-call.27
  458.5 40.2 %all-gather.11.cloned.1.call-done = bf16[8192,64]{0,1:T(8,128)(2,1)} async-done(((bf16[1024,64]{0,1:T(8,128)(2,1)}), bf16[8192,64]{0,1:T(8,128)(2,1)}) %all-gather.11.cloned.1.call-update) | async-done | bytes 1048592 | tf_op jit(solution)/shard_map/all_gather | solution.py:52
  498.7 28.4 %convolution_bitcast_fusion = f32[4096,64]{0,1:T(8,128)} fusion(bf16[8192,64]{0,1:T(8,128)(2,1)} %all-gather.11.cloned.1.call-done, bf16[4096,8192]{1,0:T(8,128)(2,1)} %param.6), kind=kOutput, calls=%fused_computation | convolution fusion | flops 4294967296 | bytes 69206016 | tf_op jit(solution)/shard_map/dot_general | solution.py:48
  527.4 24.9 %reduce-scatter.11.cloned.1.call-done = f32[1024,64]{0,1:T(8,128)} async-done(((f32[4096,64]{0,1:T(8,128)}), f32[1024,64]{0,1:T(8,128)}) %reduce-scatter.11.cloned.1.call-update) | async-done | bytes 262160 | tf_op jit(solution)/shard_map/reduce_scatter | solution.py:53
  553.3 1.7 fusion
  555.1 124.3 %all-reduce.5.cloned.1.call-done = f32[256,64]{0,1:T(8,128)} async-done(((f32[256,64]{0,1:T(8,128)}), f32[256,64]{0,1:T(8,128)}) %all-reduce.5.cloned.1.call-update) | async-done | bytes 65552 | tf_op jit(solution)/shard_map/psum | solution.py:57
  680.6 5.8 cholesky.228
  689.3 11.7 %cholesky.77 = f32[128,128]{1,0:T(8,128)S(1)} custom-call(f32[128,128]{1,0:T(8,128)S(1)} %cholesky.237), custom_call_target="Cholesky" | custom-call | tf_op jit(solution)/shard_map/jit(cholesky)/cholesky | solution.py:38
  701.1 1.8 fusion.33
  702.9 9.8 %custom-call.21 = f32[1,128,128]{1,2,0:T(8,128)S(1)} custom-call(f32[1,128,128]{2,1,0:T(8,128)S(1)} %get-tuple-element.28), custom_call_target="InvertDiagBlocksLowerTriangular" | custom-call | tf_op jit(solution)/shard_map/jit(cholesky)/cholesky | solution.py:38
  713.1 5.8 cholesky.135
  721.8 19.9 %custom-call.22 = f32[2,128,128]{1,2,0:T(8,128)S(1)} custom-call(f32[2,128,128]{2,1,0:T(8,128)S(1)} %pad_maximum_fusion.7), custom_call_target="InvertDiagBlocksLowerTriangular" | custom-call | tf_op jit(solution)/shard_map/triangular_solve | solution.py:40
  (82 shorter events, 23.3 us)
Async XLA Ops:
  6.5 98.5 %copy-start = (f32[1024,64]{0,1:T(8,128)S(1)}, f32[1024,64]{0,1:T(8,128)}, u32[]{:S(2)}) copy-start(f32[1024,64]{0,1:T(8,128)} %param.8) | copy-start | bytes 786436
  6.5 98.5 %copy-start.1 = (f32[1024,64]{0,1:T(8,128)S(1)}, f32[1024,64]{0,1:T(8,128)}, u32[]{:S(2)}) copy-start(f32[1024,64]{0,1:T(8,128)} %param.7) | copy-start | bytes 786436
  6.5 43.6 %all-gather.5.cloned.1.call-start = ((), (), s32[]{:S(2)}) async-start(), calls=%async_computation.4 | async-start | bytes 1179648 | tf_op jit(solution)/shard_map/all_gather | solution.py:52
  8.3 96.8 %reduce-scatter.5.cloned.1.call-start = ((), (), s32[]{:S(2)}) async-start(), calls=%async_computation.5 | async-start | bytes 1310720 | tf_op jit(solution)/shard_map/reduce_scatter | solution.py:53
  79.8 119.9 %all-gather.7.cloned.1.call-start = ((), (), s32[]{:S(2)}) async-start(), calls=%async_computation.6 | async-start | bytes 1179648 | tf_op jit(solution)/shard_map/all_gather | solution.py:52
  159.6 93.8 %reduce-scatter.7.cloned.1.call-start = ((), (), s32[]{:S(2)}) async-start(), calls=%async_computation.7 | async-start | bytes 1310720 | tf_op jit(solution)/shard_map/reduce_scatter | solution.py:53
  228.2 121.0 %all-gather.9.cloned.1.call-start = ((), (), s32[]{:S(2)}) async-start(), calls=%async_computation.8 | async-start | bytes 1179648 | tf_op jit(solution)/shard_map/all_gather | solution.py:52
  308.9 93.9 %reduce-scatter.9.cloned.1.call-start = ((), (), s32[]{:S(2)}) async-start(), calls=%async_computation.9 | async-start | bytes 1310720 | tf_op jit(solution)/shard_map/reduce_scatter | solution.py:53
  377.5 121.2 %all-gather.11.cloned.1.call-start = ((), (), s32[]{:S(2)}) async-start(), calls=%async_computation.10 | async-start | bytes 1179648 | tf_op jit(solution)/shard_map/all_gather | solution.py:52
  458.4 93.9 %reduce-scatter.11.cloned.1.call-start = ((), (), s32[]{:S(2)}) async-start(), calls=%async_computation.11 | async-start | bytes 1310720 | tf_op jit(solution)/shard_map/reduce_scatter | solution.py:53
  527.1 152.3 %all-reduce.5.cloned.1.call-start = ((), (), s32[]{:S(2)}) async-start(), calls=%async_computation.12 | async-start | bytes 131072 | tf_op jit(solution)/shard_map/psum | solution.py:57
Sparse Core Ops, SparseCore 0:
  9.5 40.6 all-gather.4
  79.9 25.0 reduce-scatter.4
  159.7 40.0 all-gather.6
  228.3 25.0 reduce-scatter.6
  309.0 40.0 all-gather.8
  377.6 25.0 reduce-scatter.8
  458.5 40.1 all-gather.10
  527.2 25.0 reduce-scatter.10
  557.9 121.4 all-reduce.4
where the time goes:
time: 752 us; the launch traced here: 751 us
  waiting for transfers between devices  387 us (51%)
  matrix products  134 us (18%)
  blocking collectives  117 us (16%)
  other arithmetic  96.9 us (13%)
  between operations  14.9 us (2%)
    all_gather x4, waiting for transfers between devices, operate(): partial_sum = fold_panel(lax.all_gather(operand, 'row', axis=0, tiled=True))  162 us
    psum x1, waiting for transfers between devices, reduce_all(): return lax.psum(local_sum, ('row', 'col'))  124 us
    psum x3, blocking collectives, reduce_all(): return lax.psum(local_sum, ('row', 'col'))  117 us
    dot_general x4, matrix products, fold_panel(): return jnp.dot(matrix, panel_piece, preferred_element_type=jnp.float32)  115 us
    reduce_scatter x4, waiting for transfers between devices, operate(): lax.psum_scatter(partial_sum, 'col', scatter_dimension=0, tiled=True)  100 us
    another operation x7, other arithmetic, least_squares(): lower_factor = jnp.linalg.cholesky(normal_matrix)  28.8 us
    another operation x12, other arithmetic, orthonormal(): lower_factor = jnp.linalg.cholesky(gram_sum)  26.1 us
    another operation x6, other arithmetic, least_squares(): lax.linalg.triangular_solve(lower_factor, halfway, left_side=True, lower=...  20.1 us
  transfers between devices with their start and end apart: 9, of which 9 were waited for; matrix products, arithmetic and copies ran while one was open for 0% of the time, Pallas kernels for 0%

commit v1 on v0

v1 whole, which is shorter than its diff:
```python
import functools

import jax
import jax.numpy as jnp
from jax import lax
from jax.experimental import pallas as pl
from jax.experimental.pallas import tpu as pltpu
from jax.sharding import PartitionSpec as P

STEPS = 3
DIAGONAL_SHIFT = 1.4
MESH = pl.DeviceIdType.MESH
SLOT_BYTES = 40 * 1024 * 1024
VMEM = pl.BlockSpec(memory_space=pltpu.VMEM)


def bits_of(count):
    return [1 << b for b in range(count.bit_length() - 1)]


def flipped(me, weight):
    bit = lax.rem(lax.div(me, weight), 2)
    return me + weight * (1 - 2 * bit)


def dot_high(a, b, contract=(1, 0)):
    return lax.dot_general(
        a, b, (((contract[0],), (contract[1],)), ((), ())),
        precision=lax.Precision.HIGHEST, preferred_element_type=jnp.float32,
    )


def greet(peers):
    barrier = pltpu.get_barrier_semaphore()
    for peer in peers:
        pl.semaphore_signal(barrier, inc=1, device_id=peer, device_id_type=MESH)
    pl.semaphore_wait(barrier, len(peers))


def operate_kernel(rows, cols, slots, own_ref, matrix_ref, out_ref, tiles, gathered, acc, parts, landed,
                   tile_sem, zs, zr, ys, yr, rs, rr):
    row, col = lax.axis_index("row"), lax.axis_index("col")
    width, chunk = own_ref.shape
    panel = matrix_ref.shape[0]
    half = rows // 2
    a, b = lax.div(row, 2), lax.rem(row, 2)
    partner = (a * 2 + (1 - b), col)

    def source(d):
        return lax.rem(a - d + half, half) * 2

    plan = [(0, False), (0, True)]
    for d in range(1, half):
        plan += [(d, False), (d, True)]

    def block_index(step):
        d, other = plan[step]
        return source(d) + ((1 - b) if other else b)

    def fetch(step):
        columns = pl.ds(pl.multiple_of(block_index(step) * chunk, chunk), chunk)
        return pltpu.make_async_copy(
            matrix_ref.at[:, columns], tiles.at[step % slots], tile_sem.at[step % slots]
        )

    for step in range(slots):
        fetch(step).start()

    peers = [(lax.rem(a + d, half) * 2 + b, col) for d in range(1, half)]
    greet(peers + [partner] + [(row, flipped(col, w)) for w in bits_of(cols)])

    def to_partner(d):
        src = own_ref if d == 0 else gathered.at[source(d) + b]
        return pltpu.make_async_remote_copy(
            src_ref=src, dst_ref=gathered.at[source(d) + b],
            send_sem=ys.at[d], recv_sem=yr.at[d], device_id=partner, device_id_type=MESH,
        )

    def along(d):
        return pltpu.make_async_remote_copy(
            src_ref=own_ref, dst_ref=gathered.at[row],
            send_sem=zs.at[d], recv_sem=zr.at[d], device_id=peers[d - 1], device_id_type=MESH,
        )

    to_partner(0).start()
    for d in range(1, half):
        along(d).start()

    tile_rows = min(panel, 512)

    def multiply(step):
        d, other = plan[step]
        if other:
            to_partner(d).wait_recv()
        fetch(step).wait()
        block = own_ref[...] if step == 0 else gathered[block_index(step)]
        q = block.astype(jnp.float32).T.astype(jnp.bfloat16)
        slot = step % slots

        @pl.loop(0, panel // tile_rows)
        def _(i):
            at = pl.ds(pl.multiple_of(i * tile_rows, tile_rows), tile_rows)
            product = jnp.dot(tiles[slot, at, :], q, preferred_element_type=jnp.float32)
            if step == 0:
                acc[at, :] = product
            else:
                acc[at, :] += product

        if step + slots < rows:
            fetch(step + slots).start()

    arrived = 1
    for step in range(rows):
        if step >= 1 and arrived < half:
            along(arrived).wait_recv()
            to_partner(arrived).start()
            arrived += 1
        multiply(step)

    @pl.loop(0, cols)
    def _(c):
        parts[c] = acc[pl.ds(pl.multiple_of(c * chunk, chunk), chunk), :].T

    base = 0
    sends = []
    for w in bits_of(cols):
        low, bit = lax.rem(col, w), lax.rem(lax.div(col, w), 2)
        other_col = flipped(col, w)
        count = cols // (2 * w)
        copies = []
        for j in range(count):
            copies.append(pltpu.make_async_remote_copy(
                src_ref=parts.at[low + (1 - bit) * w + j * 2 * w], dst_ref=landed.at[base + j],
                send_sem=rs.at[base + j], recv_sem=rr.at[base + j],
                device_id=(row, other_col), device_id_type=MESH,
            ))
            copies[-1].start()
        for j in range(count):
            copies[j].wait_recv()
            mine = low + bit * w + j * 2 * w
            parts[mine] = parts[mine] + landed[base + j]
        sends += copies
        base += count
    out_ref[...] = parts[col]
    for copy in sends:
        copy.wait_send()
    for d in range(half):
        to_partner(d).wait_send()
    for d in range(1, half):
        along(d).wait_send()


def operate(own, matrix, rows, cols):
    width, chunk = own.shape
    panel = matrix.shape[0]
    slots = max(1, min(rows, SLOT_BYTES // (panel * chunk * 2)))
    half = rows // 2
    landings = max(1, cols - 1)
    dma = pltpu.SemaphoreType.DMA
    return pl.pallas_call(
        functools.partial(operate_kernel, rows, cols, slots),
        out_shape=jax.ShapeDtypeStruct((width, chunk), jnp.float32),
        in_specs=[VMEM, pl.BlockSpec(memory_space=pl.ANY)],
        out_specs=VMEM,
        scratch_shapes=[
            pltpu.VMEM((slots, panel, chunk), jnp.bfloat16),
            pltpu.VMEM((rows, width, chunk), jnp.bfloat16),
            pltpu.VMEM((panel, width), jnp.float32),
            pltpu.VMEM((cols, width, chunk), jnp.float32),
            pltpu.VMEM((landings, width, chunk), jnp.float32),
            dma((slots,)), dma((half,)), dma((half,)), dma((half,)), dma((half,)),
            dma((landings,)), dma((landings,)),
        ],
        compiler_params=pltpu.CompilerParams(
            collective_id=0, has_side_effects=True, vmem_limit_bytes=60 * 1024 * 1024
        ),
        name="operate",
    )(own, matrix)


def gram_kernel(rows, cols, left_ref, right_ref, out_ref, held, landed, send_sem, recv_sem):
    row, col = lax.axis_index("row"), lax.axis_index("col")
    partners = [(row, flipped(col, w)) for w in bits_of(cols)]
    partners += [(flipped(row, w), col) for w in bits_of(rows)]
    held[0] = dot_high(left_ref[...], right_ref[...], (1, 1))
    greet(partners)
    copies = []
    for i, partner in enumerate(partners):
        copy = pltpu.make_async_remote_copy(
            src_ref=held.at[i], dst_ref=landed.at[i], send_sem=send_sem.at[i],
            recv_sem=recv_sem.at[i], device_id=partner, device_id_type=MESH,
        )
        copy.start()
        copy.wait_recv()
        total = held[i] + landed[i]
        if i + 1 < len(partners):
            held[i + 1] = total
        else:
            out_ref[...] = total
        copies.append(copy)
    for copy in copies:
        copy.wait_send()


def gram_total(left, right, rows, cols, ident):
    shape = (left.shape[0], right.shape[0])
    n = len(bits_of(rows)) + len(bits_of(cols))
    return pl.pallas_call(
        functools.partial(gram_kernel, rows, cols),
        out_shape=jax.ShapeDtypeStruct(shape, jnp.float32),
        in_specs=[VMEM, VMEM],
        out_specs=VMEM,
        scratch_shapes=[
            pltpu.VMEM((n,) + shape, jnp.float32), pltpu.VMEM((n,) + shape, jnp.float32),
            pltpu.SemaphoreType.DMA((n,)), pltpu.SemaphoreType.DMA((n,)),
        ],
        compiler_params=pltpu.CompilerParams(collective_id=ident, has_side_effects=True),
        name=f"gram{ident}",
    )(left, right)


def factor(gram):
    n = gram.shape[0]
    i = lax.broadcasted_iota(jnp.int32, (n, n), 0)
    j = lax.broadcasted_iota(jnp.int32, (n, n), 1)
    work = jnp.concatenate([gram, (i == j).astype(jnp.float32)], axis=1)
    at_row = lax.broadcasted_iota(jnp.int32, work.shape, 0)
    scale = jnp.ones((n, 1), jnp.float32)
    at = lax.broadcasted_iota(jnp.int32, (n, 1), 0)
    for k in range(n):
        pivot = work[k:k + 1, k:k + 1]
        line = work[k:k + 1, :] * (1.0 / pivot)
        scale = jnp.where(at == k, pivot, scale)
        work = work - jnp.where(at_row > k, work[:, k:k + 1] * line, 0.0)
    work = work * (1.0 / jnp.sqrt(scale))
    upper = jnp.where(j >= i, work[:, :n], 0.0)
    inverse = jnp.where(j <= i, work[:, n:], 0.0)
    return upper, inverse


def first_kernel(gram_ref, block_ref, basis_ref, upper_ref):
    upper, inverse = factor(gram_ref[...])
    upper_ref[...] = upper
    basis_ref[...] = dot_high(inverse, block_ref[...])


def step_kernel(gram_ref, block_ref, stacked_ref, basis_ref, upper_ref):
    span = stacked_ref.shape[0]
    sums = gram_ref[...]
    projected = sums[:, :span]
    upper, inverse = factor(sums[:, span:] - dot_high(projected, projected, (1, 1)))
    upper_ref[...] = upper
    cleaned = block_ref[...] - dot_high(projected, stacked_ref[...])
    basis_ref[...] = dot_high(inverse, cleaned)


def orthonormal(kernel, width, chunk, *operands):
    return pl.pallas_call(
        kernel,
        out_shape=(
            jax.ShapeDtypeStruct((width, chunk), jnp.float32),
            jax.ShapeDtypeStruct((width, width), jnp.float32),
        ),
        in_specs=[VMEM] * len(operands),
        out_specs=(VMEM, VMEM),
        name="orthonormal",
    )(*operands)


def solve_kernel(count, normal_ref, target_ref, out_ref):
    w = target_ref.shape[1]

    def cut(k):
        return slice(k * w, (k + 1) * w)

    normal = {(p, q): normal_ref[cut(p), cut(q)] for p in range(count) for q in range(p, count)}
    halfway = [target_ref[cut(p), :] for p in range(count)]
    inverses, upper = [], {}
    for p in range(count):
        _, inverse = factor(normal[p, p])
        inverses.append(inverse)
        halfway[p] = dot_high(inverse, halfway[p])
        for q in range(p + 1, count):
            upper[p, q] = dot_high(inverse, normal[p, q])
        for q in range(p + 1, count):
            halfway[q] = halfway[q] - dot_high(upper[p, q], halfway[p], (0, 0))
            for s in range(q, count):
                normal[q, s] = normal[q, s] - dot_high(upper[p, q], upper[p, s], (0, 0))
    for p in reversed(range(count)):
        value = halfway[p]
        for q in range(p + 1, count):
            value = value - dot_high(upper[p, q], out_ref[cut(q), :])
        out_ref[cut(p), :] = dot_high(inverses[p], value, (0, 0))


def least_squares(column_list, top_factor):
    width = top_factor.shape[0]
    count = len(column_list)
    pieces = []
    for position, (projected, upper_factor) in enumerate(column_list):
        filler = jnp.zeros(((count - position - 1) * width, width), jnp.float32)
        pieces.append(jnp.concatenate([projected, upper_factor, filler], axis=0))
    hessenberg = jnp.concatenate(pieces, axis=1)
    normal = dot_high(hessenberg, hessenberg, (0, 0))
    target = dot_high(hessenberg[:width], top_factor, (0, 0))
    return pl.pallas_call(
        functools.partial(solve_kernel, count),
        out_shape=jax.ShapeDtypeStruct(target.shape, jnp.float32),
        in_specs=[VMEM, VMEM],
        out_specs=VMEM,
        name="least_squares",
    )(normal, target)


def per_device(rows, cols, matrix, right_sides, initial_guess):
    guess, sides = initial_guess.T, right_sides.T
    width, chunk = guess.shape

    def apply(block):
        return DIAGONAL_SHIFT * block + operate(block.astype(jnp.bfloat16), matrix, rows, cols)

    residual = sides - apply(guess)
    gram = gram_total(residual, residual, rows, cols, 1)
    basis, top_factor = orthonormal(first_kernel, width, chunk, gram, residual)
    basis_list, column_list = [basis], []
    for iteration in range(STEPS):
        applied = apply(basis_list[-1])
        stacked = jnp.concatenate(basis_list, axis=0)
        sums = gram_total(
            applied, jnp.concatenate([stacked, applied], axis=0), rows, cols, 2 + iteration
        )
        basis, upper = orthonormal(step_kernel, width, chunk, sums, applied, stacked)
        basis_list.append(basis)
        column_list.append((sums[:, : stacked.shape[0]].T, upper))
    coefficients = least_squares(column_list, top_factor)
    return initial_guess + dot_high(stacked, coefficients, (0, 0))


def solution(mesh):
    return jax.shard_map(
        functools.partial(per_device, mesh.shape["row"], mesh.shape["col"]),
        mesh=mesh,
        in_specs=(P("row", "col"), P(("row", "col"), None), P(("row", "col"), None)),
        out_specs=P(("row", "col"), None),
        check_vma=False,
    )
```

time: 752 us -> 343 us (0.46)
  waiting for transfers between devices: 387 us -> 0 us
  Pallas kernels: 0 us -> 317 us
  matrix products: 134 us -> 4.5 us
  blocking collectives: 117 us -> 0 us
  other arithmetic: 96.9 us -> 15.3 us
  between operations: 14.9 us -> 0.25 us
    pallas_call x0 -> x13, Pallas kernels: none -> 317 us  [the longest x4 195 us: operate(): pl.pallas_call(functools.partial(operate_kernel, rows, cols, slots), out_...]
    all_gather x4 -> x0, waiting for transfers between devices: 162 us -> none  [operate(): partial_sum = fold_panel(lax.all_gather(operand, 'row', axis=0, tiled=True))]
    psum x1 -> x0, waiting for transfers between devices: 124 us -> none  [reduce_all(): return lax.psum(local_sum, ('row', 'col'))]
    dot_general x16 -> x3, matrix products: 128 us -> 4.5 us  [dot_high(): lax.dot_general(a, b, (((contract[0],), (contract[1],)), ((), ())), preci...]
    psum x3 -> x0, blocking collectives: 117 us -> none  [reduce_all(): return lax.psum(local_sum, ('row', 'col'))]
    reduce_scatter x4 -> x0, waiting for transfers between devices: 100 us -> none  [operate(): lax.psum_scatter(partial_sum, 'col', scatter_dimension=0, tiled=True)]
    another operation x29 -> x0, other arithmetic: 90.3 us -> none  [the longest x7 28.8 us: least_squares(): lower_factor = jnp.linalg.cholesky(normal_matrix)]
  transfers between devices with their start and end apart: 9 -> 0, of which waited for: 9 -> 0; matrix products, arithmetic and copies ran while one was open for 0% -> 0% of each run, Pallas kernels for 0% -> 0%
where the time goes in v1:
time: 343 us; the launch traced here: 339 us
  Pallas kernels  317 us (92%)
  other arithmetic  15.3 us (4%)
  matrix products  4.5 us (1%)
    pallas_call x4, Pallas kernels, operate(): pl.pallas_call(functools.partial(operate_kernel, rows, cols, slots), out_...  195 us
    pallas_call x4, Pallas kernels, gram_total(): pl.pallas_call(functools.partial(gram_kernel, rows, cols), out_shape=jax....  68.5 us
    pallas_call x4, Pallas kernels, orthonormal(): pl.pallas_call(kernel, out_shape=(jax.ShapeDtypeStruct((width, chunk), jn...  32.2 us
    pallas_call x1, Pallas kernels, least_squares(): pl.pallas_call(functools.partial(solve_kernel, count), out_shape=jax.Shap...  20.7 us

profile of v1, /device:TPU:1, one launch (start us, length us, event | category | flops | bytes accessed | tf_op | source)
XLA Modules:
  0.0 338.6 jit_solution(13857798757453889751)
XLA Ops:
  0.0 1.7 convert_bitcast_fusion.own_ref
  1.7 48.2 %operate.4 = f32[64,1024]{1,0:T(8,128)} custom-call(bf16[64,1024]{1,0:T(8,128)(2,1)} %convert_bitcast_fusion.own_ref, bf16[4096,8192]{1,0:T(8,128)(2,1)} %matrix_ref.7), custom_call_target="tpu_custom_call" | custom-call | tf_op jit(solution)/shard_map/operate/pallas_call | solution.py:160
  49.9 1.7 fusion.left_ref.right_ref.block_ref
  51.6 15.9 %gram1.1.gram_ref = f32[64,64]{1,0:T(8,128)} custom-call(f32[64,1024]{1,0:T(8,128)} %fusion.left_ref.right_ref.block_ref, f32[64,1024]{1,0:T(8,128)} %fusion.left_ref.right_ref.block_ref), custom_call_target="tpu_custom_call" | custom-call | tf_op jit(solution)/shard_map/gram1/pallas_call | solution.py:208
  67.6 7.7 %orthonormal.4 = (f32[64,1024]{1,0:T(8,128)}, f32[64,64]{1,0:T(8,128)}) custom-call(f32[64,64]{1,0:T(8,128)} %gram1.1.gram_ref, f32[64,1024]{1,0:T(8,128)} %fusion.left_ref.right_ref.block_ref), custom_call_target="tpu_custom_call" | custom-call | tf_op jit(solution)/shard_map/orthonormal/pallas_call | solution.py:258
  75.3 1.7 convert_element_type.16.own_ref
  77.0 48.7 %operate.5 = f32[64,1024]{1,0:T(8,128)} custom-call(bf16[64,1024]{1,0:T(8,128)(2,1)} %convert_element_type.16.own_ref, bf16[4096,8192]{1,0:T(8,128)(2,1)} %matrix_ref.7), custom_call_target="tpu_custom_call" | custom-call | tf_op jit(solution)/shard_map/operate/pallas_call | solution.py:160
  125.7 1.0 multiply_add_fusion.2
  126.7 0.9 pad_maximum_fusion.3.right_ref
  127.6 16.0 %gram2.1.gram_ref = f32[64,128]{1,0:T(8,128)} custom-call(f32[64,1024]{1,0:T(8,128)} %copy-done.5, f32[128,1024]{1,0:T(8,128)} %pad_maximum_fusion.3.right_ref), custom_call_target="tpu_custom_call" | custom-call | tf_op jit(solution)/shard_map/gram2/pallas_call | solution.py:208
  143.6 8.1 %orthonormal.5 = (f32[64,1024]{1,0:T(8,128)}, f32[64,64]{1,0:T(8,128)}) custom-call(f32[64,128]{1,0:T(8,128)} %gram2.1.gram_ref, f32[64,1024]{1,0:T(8,128)} %copy-done.5, f32[64,1024]{1,0:T(8,128)} %get-tuple-element.12.stacked_ref), custom_call_target="tpu_custom_call" | custom-call | tf_op jit(solution)/shard_map/orthonormal/pallas_call | solution.py:258
  151.7 1.7 convert_element_type.17.own_ref
  153.4 48.8 %operate.6 = f32[64,1024]{1,0:T(8,128)} custom-call(bf16[64,1024]{1,0:T(8,128)(2,1)} %convert_element_type.17.own_ref, bf16[4096,8192]{1,0:T(8,128)(2,1)} %matrix_ref.7), custom_call_target="tpu_custom_call" | custom-call | tf_op jit(solution)/shard_map/operate/pallas_call | solution.py:160
  202.2 1.0 multiply_add_fusion.1
  203.2 0.9 pad_maximum_fusion.1.right_ref
  204.2 17.6 %gram3.1.gram_ref = f32[64,192]{1,0:T(8,128)} custom-call(f32[64,1024]{1,0:T(8,128)} %copy-done.4, f32[192,1024]{1,0:T(8,128)} %pad_maximum_fusion.1.right_ref), custom_call_target="tpu_custom_call" | custom-call | tf_op jit(solution)/shard_map/gram3/pallas_call | solution.py:208
  221.8 0.8 pad_maximum_fusion.2.stacked_ref
  222.7 8.0 %orthonormal.6 = (f32[64,1024]{1,0:T(8,128)}, f32[64,64]{1,0:T(8,128)}) custom-call(f32[64,192]{1,0:T(8,128)} %gram3.1.gram_ref, f32[64,1024]{1,0:T(8,128)} %copy-done.4, f32[128,1024]{1,0:T(8,128)} %pad_maximum_fusion.2.stacked_ref), custom_call_target="tpu_custom_call" | custom-call | tf_op jit(solution)/shard_map/orthonormal/pallas_call | solution.py:258
  230.7 1.7 convert_element_type.18.own_ref
  232.4 49.5 %operate.7 = f32[64,1024]{1,0:T(8,128)} custom-call(bf16[64,1024]{1,0:T(8,128)(2,1)} %convert_element_type.18.own_ref, bf16[4096,8192]{1,0:T(8,128)(2,1)} %matrix_ref.7), custom_call_target="tpu_custom_call" | custom-call | tf_op jit(solution)/shard_map/operate/pallas_call | solution.py:160
  282.0 1.0 multiply_add_fusion
  283.0 1.2 pad_maximum_fusion.right_ref
  284.2 19.0 %gram4.1.gram_ref = f32[64,256]{1,0:T(8,128)} custom-call(f32[64,1024]{1,0:T(8,128)} %copy-done.6, f32[256,1024]{1,0:T(8,128)} %pad_maximum_fusion.right_ref), custom_call_target="tpu_custom_call" | custom-call | tf_op jit(solution)/shard_map/gram4/pallas_call | solution.py:208
  303.1 8.3 %orthonormal.7 = (f32[64,1024]{1,0:T(8,128)}, f32[64,64]{1,0:T(8,128)}) custom-call(f32[64,256]{1,0:T(8,128)} %gram4.1.gram_ref, f32[64,1024]{1,0:T(8,128)} %copy-done.6, f32[192,1024]{1,0:T(8,128)} %copy-done.3), custom_call_target="tpu_custom_call" | custom-call | tf_op jit(solution)/shard_map/orthonormal/pallas_call | solution.py:258
  311.5 0.8 copy.6
  312.3 0.9 slice_bitcast_fusion
  313.2 0.1 copy.5
  313.3 0.1 copy.4
  313.4 1.1 fusion.1.normal_ref
  314.5 0.9 fusion.17.target_ref
  315.4 20.7 %least_squares.1 = f32[192,64]{1,0:T(8,128)} custom-call(f32[192,192]{1,0:T(8,128)} %fusion.1.normal_ref, f32[192,64]{1,0:T(8,128)} %fusion.17.target_ref), custom_call_target="tpu_custom_call" | custom-call | tf_op jit(solution)/shard_map/least_squares/pallas_call | solution.py:306
  336.1 2.5 convolution_add_fusion
  (34 shorter events, 0.1 us)
Async XLA Ops:
  0.0 49.9 %copy-start.7 = (f32[1024,64]{0,1:T(8,128)S(1)}, f32[1024,64]{0,1:T(8,128)}, u32[]{:S(2)}) copy-start(f32[1024,64]{0,1:T(8,128)} %param.5) | copy-start | bytes 786436
  0.0 49.9 %copy-start.11 = (f32[1024,64]{0,1:T(8,128)S(1)}, f32[1024,64]{0,1:T(8,128)}, u32[]{:S(2)}) copy-start(f32[1024,64]{0,1:T(8,128)} %param.4) | copy-start | bytes 786436
  75.3 50.4 %copy-start = (f32[64,1024]{1,0:T(8,128)S(1)}, f32[64,1024]{1,0:T(8,128)}, u32[]{:S(2)}) copy-start(f32[64,1024]{1,0:T(8,128)} %get-tuple-element.12.stacked_ref) | copy-start | bytes 786436
  77.0 126.3 %copy-start.1 = (f32[64,1024]{1,0:T(8,128)S(1)}, f32[64,1024]{1,0:T(8,128)}, u32[]{:S(2)}) copy-start(f32[64,1024]{1,0:T(8,128)} %get-tuple-element.12.stacked_ref) | copy-start | bytes 786436
  126.7 0.9 copy-start.5
  151.7 50.5 %copy-start.2 = (f32[64,1024]{1,0:T(8,128)S(1)}, f32[64,1024]{1,0:T(8,128)}, u32[]{:S(2)}) copy-start(f32[64,1024]{1,0:T(8,128)} %get-tuple-element.13) | copy-start | bytes 786436
  153.4 159.9 %copy-start.12 = (f32[64,64]{1,0:T(8,128)S(1)}, f32[64,64]{1,0:T(8,128)}, u32[]{:S(2)}) copy-start(f32[64,64]{1,0:T(8,128)} %get-tuple-element.15) | copy-start | bytes 49156
  153.4 160.0 %copy-start.10 = (f32[64,128]{1,0:T(8,128)S(1)}, f32[64,128]{1,0:T(8,128)}, u32[]{:S(2)}) copy-start(f32[64,128]{1,0:T(8,128)} %gram2.1.gram_ref) | copy-start | bytes 98308
  153.4 161.1 %copy-start.14 = (f32[64,64]{1,0:T(8,128)S(1)}, f32[64,64]{1,0:T(8,128)}, u32[]{:S(2)}) copy-start(f32[64,64]{1,0:T(8,128)} %get-tuple-element.18) | copy-start | bytes 49156
  203.2 1.0 copy-start.4
  221.8 91.4 %copy-start.9 = (f32[64,192]{1,0:T(8,128)S(1)}, f32[64,192]{1,0:T(8,128)}, u32[]{:S(2)}) copy-start(f32[64,192]{1,0:T(8,128)} %gram3.1.gram_ref) | copy-start | bytes 147460
  230.7 51.2 %copy-start.8 = (f32[64,1024]{1,0:T(8,128)S(1)}, f32[64,1024]{1,0:T(8,128)}, u32[]{:S(2)}) copy-start(f32[64,1024]{1,0:T(8,128)} %get-tuple-element.14) | copy-start | bytes 786436
  230.7 82.4 %copy-start.13 = (f32[64,64]{1,0:T(8,128)S(1)}, f32[64,64]{1,0:T(8,128)}, u32[]{:S(2)}) copy-start(f32[64,64]{1,0:T(8,128)} %get-tuple-element.16) | copy-start | bytes 49156
  283.0 1.2 copy-start.6
  283.0 20.2 %copy-start.3 = (f32[192,1024]{1,0:T(8,128)}, f32[192,1024]{1,0:T(8,128)S(1)}, u32[]{:S(2)}) copy-start(f32[192,1024]{1,0:T(8,128)S(1)} %get-tuple-element.20.stacked_ref) | copy-start | bytes 2359300
